TPU v7x, 8 devices: a whole 2x2x1 slice. The times are simulated.
8 devices in a mesh: rep: 1 (over z), dp: 8 (over x, y, core).
Axes of the slice: x: 2, y: 2, z: 1, core: 2. Of those that a mesh axis runs over, the one named last changes fastest.
Arguments:
- x: bfloat16 [8, 2048, 1280], P(('rep', 'dp'))
- dy: bfloat16 [8, 2048, 1280], P(('rep', 'dp'))
- w_gate: bfloat16 [2, 1280, 4096], replicated
- w_up: bfloat16 [2, 1280, 4096], replicated
- w_down: bfloat16 [2, 4096, 1280], replicated
- m_w_gate: float32 [2, 1280, 4096], P(None, 'dp')
- m_w_up: float32 [2, 1280, 4096], P(None, 'dp')
- m_w_down: float32 [2, 4096, 1280], P(None, 'dp')
- v_w_gate: float32 [2, 1280, 4096], P(None, 'dp')
- v_w_up: float32 [2, 1280, 4096], P(None, 'dp')
- v_w_down: float32 [2, 4096, 1280], P(None, 'dp')
Outputs:
- output 1: bfloat16 [2, 1280, 4096], P('rep')
- output 2: bfloat16 [2, 1280, 4096], P('rep')
- output 3: bfloat16 [2, 4096, 1280], P('rep')
- output 4: float32 [2, 1280, 4096], P('rep', 'dp')
- output 5: float32 [2, 1280, 4096], P('rep', 'dp')
- output 6: float32 [2, 4096, 1280], P('rep', 'dp')
- output 7: float32 [2, 1280, 4096], P('rep', 'dp')
- output 8: float32 [2, 1280, 4096], P('rep', 'dp')
- output 9: float32 [2, 4096, 1280], P('rep', 'dp')
All inputs are finite; a program needn't handle non-finite values.
Results may differ from a plain program's by a relative error of at most 0.022.
Values are sent between devices in bfloat16 or wider.
A program may use at most 2 GiB of HBM per device.

v0:
```python
import jax
import jax.numpy as jnp
from jax import lax

NAMES = ("w_gate", "w_up", "w_down")


def matmul(a, w):
    return jnp.dot(a, w, preferred_element_type=jnp.float32).astype(jnp.bfloat16)


def normed(h):
    wide = h.astype(jnp.float32)
    scale = lax.rsqrt(jnp.mean(wide**2, -1, keepdims=True) + 1e-6)
    return (wide * scale).astype(jnp.bfloat16)


def layer(h, w):
    a = normed(h)
    gate = jnp.dot(a, w["w_gate"], preferred_element_type=jnp.float32)
    up = jnp.dot(a, w["w_up"], preferred_element_type=jnp.float32)
    return h + matmul((jax.nn.silu(gate) * up).astype(jnp.bfloat16), w["w_down"])


def adamw(w, m, v, g):
    m = 0.9 * m + 0.1 * g
    v = 0.95 * v + 0.05 * g * g
    step = m * lax.rsqrt(v + 1e-8) + 0.1 * w
    return (w - 0.02 * step).astype(jnp.bfloat16), m, v


def stack(weights, h):
    for number in range(weights["w_gate"].shape[0]):
        h = layer(h, {name: w[number] for name, w in weights.items()})
    return h


def solution(mesh):
    groups = mesh.shape["rep"]

    def step(x, dy, *arrays):
        weights, m, v = (arrays[i : i + 3] for i in (0, 3, 6))
        x, dy = (t.reshape(groups, -1, *t.shape[1:]) for t in (x, dy))

        def of_a_group(x, dy):
            _, back = jax.vjp(lambda w: stack(w, x), dict(zip(NAMES, weights, strict=True)))
            by_weights = back(dy)[0]
            gradients = [by_weights[name].astype(jnp.float32) for name in NAMES]
            new = [adamw(w.astype(jnp.float32), m, v, g) for w, m, v, g in zip(weights, m, v, gradients, strict=True)]
            return tuple(one[which] for which in range(3) for one in new)

        return tuple(t.reshape(-1, *t.shape[2:]) for t in jax.vmap(of_a_group)(x, dy))

    return step
```

profile of v0, /device:TPU:0, one launch (start us, length us, event | category | flops | bytes accessed | tf_op | source)
XLA Modules:
  0.0 1520.7 jit_solution(5073762667776064248)
XLA Ops:
  10.8 8.0 copy
  18.8 29.3 %fusion.54 = f32[2048,4096]{1,0:T(8,128)} fusion(bf16[2,1280,4096]{2,1,0:T(8,128)(2,1)} %param, bf16[1,2048,1280]{2,1,0:T(8,128)(2,1)} %param.4, f32[2048]{0:T(1024)S(1)} %add_rsqrt_fusion), kind=kOutput, calls=%fused_computation.71 | convolution fusion | flops 21482700800 | bytes 49291264 | tf_op jit(solution)/vmap(jvp())/dot_general | solution.py:20
  48.2 27.7 %fusion.52 = f32[2048,4096]{1,0:T(8,128)} fusion(bf16[2,1280,4096]{2,1,0:T(8,128)(2,1)} %param.5, bf16[1,2048,1280]{2,1,0:T(8,128)(2,1)S(1)} %bitcast.360, f32[2048]{0:T(1024)S(1)} %add_rsqrt_fusion), kind=kOutput, calls=%fused_computation.69 | convolution fusion | flops 21482700800 | bytes 49291264 | tf_op jit(solution)/vmap(jvp())/dot_general | solution.py:21
  75.8 27.5 %fusion.26 = bf16[2048,4096]{1,0:T(8,128)(2,1)} fusion(f32[2048,4096]{1,0:T(8,128)} %fusion.52, f32[2048,4096]{1,0:T(8,128)} %fusion.54), kind=kLoop, calls=%fused_computation.39 | loop fusion | flops 50331648 | bytes 83886080
  103.4 30.2 %fusion.39 = (f32[2048]{0:T(1024)S(1)}, bf16[1,2048,1280]{1,2,0:T(8,128)(2,1)}) fusion(bf16[1,2048,1280]{1,2,0:T(8,128)(2,1)} %copy, bf16[2048,4096]{1,0:T(8,128)(2,1)} %fusion.26, bf16[2,4096,1280]{2,1,0:T(8,128)(2,1)} %param.3), kind=kOutput, calls=%fused_computation.56 | convolution fusion | flops 21487941632 | bytes 37756928 | tf_op jit(solution)/vmap(jvp())/dot_general | solution.py:9
  134.2 29.8 %fusion.42 = f32[2048,4096]{1,0:T(8,128)} fusion(bf16[2,1280,4096]{2,1,0:T(8,128)(2,1)} %param, bf16[1,2048,1280]{1,2,0:T(8,128)(2,1)} %get-tuple-element.10, f32[2048]{0:T(1024)S(1)} %bitcast.364), kind=kOutput, calls=%fused_computation.59 | convolution fusion | flops 21482700800 | bytes 49291264 | tf_op jit(solution)/vmap(jvp())/dot_general | solution.py:20
  164.0 28.3 %fusion.46 = f32[2048,4096]{1,0:T(8,128)} fusion(bf16[2,1280,4096]{2,1,0:T(8,128)(2,1)} %param.5, bf16[1,2048,1280]{1,2,0:T(8,128)(2,1)S(1)} %copy-done.1, f32[2048]{0:T(1024)S(1)} %bitcast.365), kind=kOutput, calls=%fused_computation.63 | convolution fusion | flops 21482700800 | bytes 49291264 | tf_op jit(solution)/vmap(jvp())/dot_general | solution.py:21
  192.3 28.9 %convolution_convert_fusion.1 = bf16[2048,4096]{1,0:T(8,128)(2,1)} fusion(bf16[2,4096,1280]{2,1,0:T(8,128)(2,1)} %param.3, bf16[1,2048,1280]{2,1,0:T(8,128)(2,1)} %param.2), kind=kOutput, calls=%fused_computation.48 | convolution fusion | flops 21483225088 | bytes 32505856 | tf_op jit(solution)/vmap(transpose(jvp()))/dot_general | solution.py:9
  229.1 32.9 %fusion.6 = bf16[2048,4096]{1,0:T(8,128)(2,1)} fusion(f32[2048,4096]{1,0:T(8,128)} %fusion.42, f32[2048,4096]{1,0:T(8,128)} %fusion.46, bf16[2048,4096]{1,0:T(8,128)(2,1)} %convolution_convert_fusion.1), kind=kLoop, calls=%fused_computation.11 | loop fusion | flops 100663296 | bytes 100663296
  262.0 29.0 %fusion.69 = bf16[2048,1280]{0,1:T(8,128)(2,1)} fusion(bf16[2048,4096]{1,0:T(8,128)(2,1)} %fusion.6, bf16[2,1280,4096]{2,1,0:T(8,128)(2,1)} %param), kind=kOutput, calls=%fused_computation.87 | convolution fusion | flops 21474836480 | bytes 32505856 | tf_op jit(solution)/vmap(transpose(jvp()))/dot_general | solution.py:20
  291.1 43.5 %fusion.41 = (f32[2048]{0:T(1024)S(1)}, bf16[1,2048,1280]{1,2,0:T(8,128)(2,1)}) fusion(bf16[1,2048,1280]{1,2,0:T(8,128)(2,1)} %get-tuple-element.10, bf16[2048,1280]{0,1:T(8,128)(2,1)} %fusion.69, bf16[2,1280,4096]{2,1,0:T(8,128)(2,1)} %param.5, bf16[2048,4096]{1,0:T(8,128)(2,1)} %convolution_convert_fusion.1, f32[2048,4096]{1,0:T(8,128)} %fusion.42), kind=kOutput, calls=%fused_computation.58 | convolution fusion | flops 21540894720 | bytes 76554240 | tf_op jit(solution)/vmap(transpose(jvp()))/dot_general | solution.py:21
  334.6 12.4 fusion.116
  347.0 28.8 %fusion.140 = f32[1280,4096]{0,1:T(8,128)} fusion(bf16[2048,1280]{0,1:T(8,128)(2,1)} %fusion.116, bf16[2048,4096]{1,0:T(8,128)(2,1)} %fusion.26), kind=kOutput, calls=%fused_computation.153 | convolution fusion | flops 21474836480 | bytes 42991616 | tf_op jit(solution)/vmap(transpose(jvp()))/dot_general | solution.py:9
  375.9 37.3 %fusion.28 = f32[4096,1280]{1,0:T(8,128)} fusion(f32[2048,4096]{1,0:T(8,128)} %fusion.46, f32[2048,4096]{1,0:T(8,128)} %fusion.42, bf16[1,2048,1280]{2,1,0:T(8,128)(2,1)} %param.2), kind=kOutput, calls=%fused_computation.41 | convolution fusion | flops 21525168128 | bytes 93323264 | tf_op jit(solution)/vmap(transpose(jvp()))/dot_general | solution.py:9
  413.3 29.5 %convolution_convert_fusion = bf16[2048,4096]{1,0:T(8,128)(2,1)} fusion(bf16[2048,1280]{0,1:T(8,128)(2,1)} %fusion.116, bf16[2,4096,1280]{2,1,0:T(8,128)(2,1)} %param.3), kind=kOutput, calls=%fused_computation.47 | convolution fusion | flops 21483225088 | bytes 32505856 | tf_op jit(solution)/vmap(transpose(jvp()))/dot_general | solution.py:9
  442.9 33.2 %fusion.2 = f32[4096,1280]{0,1:T(8,128)} fusion(bf16[2048,4096]{1,0:T(8,128)(2,1)} %convolution_convert_fusion, f32[2048,4096]{1,0:T(8,128)} %fusion.54, bf16[1,2048,1280]{2,1,0:T(8,128)(2,1)} %param.4, f32[2048]{0:T(1024)S(1)} %copy-done.8), kind=kOutput, calls=%fused_computation.8 | convolution fusion | flops 21533032448 | bytes 76554240 | tf_op jit(solution)/vmap(transpose(jvp()))/dot_general | solution.py:21
  476.8 32.6 %fusion.22 = f32[4096,1280]{0,1:T(8,128)} fusion(bf16[2048,4096]{1,0:T(8,128)(2,1)} %convolution_convert_fusion.1, f32[2048,4096]{1,0:T(8,128)} %fusion.42, bf16[1,2048,1280]{1,2,0:T(8,128)(2,1)} %get-tuple-element.10, f32[2048]{0:T(1024)S(1)} %bitcast.367), kind=kOutput, calls=%fused_computation.33 | convolution fusion | flops 21533032448 | bytes 76554240 | tf_op jit(solution)/vmap(transpose(jvp()))/dot_general | solution.py:21
  509.5 28.6 %fusion.121 = f32[4096,1280]{0,1:T(8,128)} fusion(bf16[2048,4096]{1,0:T(8,128)(2,1)} %fusion.6, bf16[1,2048,1280]{1,2,0:T(8,128)(2,1)} %get-tuple-element.10, f32[2048]{0:T(1024)S(1)} %bitcast.368), kind=kOutput, calls=%fused_computation.129 | convolution fusion | flops 21482700800 | bytes 42999808 | tf_op jit(solution)/vmap(transpose(jvp()))/dot_general | solution.py:20
  538.2 46.6 %fusion.10 = f32[4096,1280]{0,1:T(8,128)} fusion(f32[2048,4096]{1,0:T(8,128)} %fusion.54, f32[2048,4096]{1,0:T(8,128)} %fusion.52, bf16[2048,4096]{1,0:T(8,128)(2,1)} %convolution_convert_fusion, bf16[1,2048,1280]{2,1,0:T(8,128)(2,1)} %param.4, f32[2048]{0:T(1024)S(1)} %copy-done.8), kind=kOutput, calls=%fused_computation.15 | convolution fusion | flops 21574975488 | bytes 110108672 | tf_op jit(solution)/vmap(transpose(jvp()))/dot_general | solution.py:20
  586.8 49.4 %reduce-scatter.27.cloned.1.call-done = f32[512,1280]{1,0:T(8,128)} async-done(((f32[4096,1280]{1,0:T(8,128)}), f32[512,1280]{1,0:T(8,128)}) %reduce-scatter.27.cloned.1.call-update) | async-done | bytes 2621456
  638.1 9.2 fusion.128
  647.3 119.9 %reduce-scatter.25.cloned.1.call-done = f32[4096,160]{0,1:T(8,128)} async-done(((f32[4096,1280]{0,1:T(8,128)}), f32[4096,160]{0,1:T(8,128)}) %reduce-scatter.25.cloned.1.call-update) | async-done | bytes 2621456
  769.1 128.4 %reduce-scatter.23.cloned.1.call-done = f32[4096,160]{0,1:T(8,128)} async-done(((f32[4096,1280]{0,1:T(8,128)}), f32[4096,160]{0,1:T(8,128)}) %reduce-scatter.23.cloned.1.call-update) | async-done | bytes 2621456
  899.5 9.2 fusion.129
  908.7 119.7 %reduce-scatter.19.cloned.1.call-done = f32[4096,160]{0,1:T(8,128)} async-done(((f32[4096,1280]{0,1:T(8,128)}), f32[4096,160]{0,1:T(8,128)}) %reduce-scatter.19.cloned.1.call-update) | async-done | bytes 2621456
  1030.3 129.0 %reduce-scatter.21.cloned.1.call-done = f32[4096,160]{0,1:T(8,128)} async-done(((f32[4096,1280]{0,1:T(8,128)}), f32[4096,160]{0,1:T(8,128)}) %reduce-scatter.21.cloned.1.call-update) | async-done | bytes 2621456
  1161.2 9.3 fusion.130
  1170.5 92.5 %all-gather.14.cloned.1.call-done = bf16[1,2,4096,1280]{3,2,1,0:T(8,128)(2,1)} async-done(((bf16[1,2,512,1280]{3,2,1,0:T(8,128)(2,1)}), bf16[1,2,4096,1280]{3,2,1,0:T(8,128)(2,1)}) %all-gather.14.cloned.1.call-update) | async-done | bytes 20971536 | tf_op jit(solution)/reshape | solution.py:52
  1263.0 104.3 %all-gather.12.cloned.1.call-done = bf16[1,2,1280,4096]{3,2,1,0:T(8,128)(2,1)} async-done(((bf16[1,2,160,4096]{3,2,1,0:T(8,128)(2,1)}), bf16[1,2,1280,4096]{3,2,1,0:T(8,128)(2,1)}) %all-gather.12.cloned.1.call-update) | async-done | bytes 20971536 | tf_op jit(solution)/reshape | solution.py:52
  1367.3 104.3 %all-gather.10.cloned.1.call-done = bf16[1,2,1280,4096]{3,2,1,0:T(8,128)(2,1)} async-done(((bf16[1,2,160,4096]{3,2,1,0:T(8,128)(2,1)}), bf16[1,2,1280,4096]{3,2,1,0:T(8,128)(2,1)}) %all-gather.10.cloned.1.call-update) | async-done | bytes 20971536 | tf_op jit(solution)/reshape | solution.py:52
  1471.6 21.1 %copy.7 = bf16[2,1280,4096]{2,1,0:T(8,128)(2,1)} copy(bf16[2,1280,4096]{2,1,0:T(8,128)(2,1)} %bitcast.358) | data formatting | bytes 41943040
  1492.8 10.6 copy.8
  (66 shorter events, 35.0 us)
Async XLA Ops:
  7.2 577.8 %reduce-scatter.29.cloned.1.call-start = ((), (), s32[]{:S(2)}) async-start(), calls=%async_computation.14 | async-start | bytes 23592960
  10.8 37.4 %slice-start.5 = ((s8[5242880]{0:T(1024)(128)(4,1)}), s8[1048576]{0:T(1024)(128)(4,1)S(1)}, s32[]{:S(2)}) async-start(s8[5242880]{0:T(1024)(128)(4,1)} %bitcast.359), calls=%async_computation.20 | async-start | bytes 2097152
  18.8 29.4 %copy-start.7 = (f32[2048]{0:T(1024)}, f32[2048]{0:T(1024)S(1)}, u32[]{:S(2)}) copy-start(f32[2048]{0:T(1024)S(1)} %add_rsqrt_fusion) | copy-start | bytes 24580
  18.8 29.4 %slice-start.6 = ((s8[5242880]{0:T(1024)(128)(4,1)}), s8[4194304]{0:T(1024)(128)(4,1)S(1)}, s32[]{:S(2)}) async-start(s8[5242880]{0:T(1024)(128)(4,1)} %bitcast.359), calls=%async_computation.21 | async-start | bytes 8388608
  133.6 0.6 copy-start.2
  133.6 30.4 %copy-start.4 = (f32[1,2048]{1,0:T(1,128)}, f32[1,2048]{1,0:T(1,128)S(1)}, u32[]{:S(2)}) copy-start(f32[1,2048]{1,0:T(1,128)S(1)} %rsqrt.29) | copy-start | bytes 24580
  134.2 29.8 %copy-start.1 = (bf16[1,2048,1280]{1,2,0:T(8,128)(2,1)S(1)}, bf16[1,2048,1280]{1,2,0:T(8,128)(2,1)}, u32[]{:S(2)}) copy-start(bf16[1,2048,1280]{1,2,0:T(8,128)(2,1)} %get-tuple-element.10) | copy-start | bytes 15728644
  291.1 43.5 %copy-start.3 = (f32[2048]{0:T(1024)S(1)}, f32[2048]{0:T(1024)}, u32[]{:S(2)}) copy-start(f32[2048]{0:T(1024)} %copy-done.2) | copy-start | bytes 24580
  291.1 43.6 %copy-start.5 = (f32[1,2048]{1,0:T(1,128)S(1)}, f32[1,2048]{1,0:T(1,128)}, u32[]{:S(2)}) copy-start(f32[1,2048]{1,0:T(1,128)} %copy-done.4) | copy-start | bytes 24580
  375.9 260.3 %reduce-scatter.27.cloned.1.call-start = ((), (), s32[]{:S(2)}) async-start(), calls=%async_computation.13 | async-start | bytes 23592960
  413.3 29.6 %copy-start.8 = (f32[2048]{0:T(1024)S(1)}, f32[2048]{0:T(1024)}, u32[]{:S(2)}) copy-start(f32[2048]{0:T(1024)} %copy-done.7) | copy-start | bytes 24580
  413.3 354.0 %reduce-scatter.25.cloned.1.call-start = ((), (), s32[]{:S(2)}) async-start(), calls=%async_computation.12 | async-start | bytes 23592960
  476.1 0.7 copy-start.6
  476.1 421.4 %reduce-scatter.23.cloned.1.call-start = ((), (), s32[]{:S(2)}) async-start(), calls=%async_computation.11 | async-start | bytes 23592960
  509.5 518.9 %reduce-scatter.19.cloned.1.call-start = ((), (), s32[]{:S(2)}) async-start(), calls=%async_computation.9 | async-start | bytes 23592960
  538.2 621.1 %reduce-scatter.21.cloned.1.call-start = ((), (), s32[]{:S(2)}) async-start(), calls=%async_computation.10 | async-start | bytes 23592960
  584.9 678.2 %all-gather.14.cloned.1.call-start = ((), (), s32[]{:S(2)}) async-start(), calls=%async_computation.8 | async-start | bytes 23592960 | tf_op jit(solution)/reshape | solution.py:52
  647.3 720.0 %all-gather.12.cloned.1.call-start = ((), (), s32[]{:S(2)}) async-start(), calls=%async_computation.7 | async-start | bytes 23592960 | tf_op jit(solution)/reshape | solution.py:52
  908.7 563.0 %all-gather.10.cloned.1.call-start = ((), (), s32[]{:S(2)}) async-start(), calls=%async_computation.6 | async-start | bytes 23592960 | tf_op jit(solution)/reshape | solution.py:52
  1471.6 21.1 %copy-start = (bf16[1,2,1280,4096]{3,2,1,0:T(8,128)(2,1)S(1)}, bf16[1,2,1280,4096]{3,2,1,0:T(8,128)(2,1)}, u32[]{:S(2)}) copy-start(bf16[1,2,1280,4096]{3,2,1,0:T(8,128)(2,1)} %all-gather.12.cloned.1.call-done) | copy-start | bytes 62914564
  1471.6 31.7 %slice-start = ((s8[20971520]{0:T(1024)(128)(4,1)}), s8[4194304]{0:T(1024)(128)(4,1)S(1)}, s32[]{:S(2)}) async-start(s8[20971520]{0:T(1024)(128)(4,1)} %bitcast.354), calls=%async_computation.15 | async-start | bytes 8388608
  1471.6 31.7 %slice-start.1 = ((s8[20971520]{0:T(1024)(128)(4,1)}), s8[4194304]{0:T(1024)(128)(4,1)S(1)}, s32[]{:S(2)}) async-start(s8[20971520]{0:T(1024)(128)(4,1)} %bitcast.354), calls=%async_computation.16 | async-start | bytes 8388608
  1471.6 31.7 %slice-start.2 = ((s8[20971520]{0:T(1024)(128)(4,1)}), s8[4194304]{0:T(1024)(128)(4,1)S(1)}, s32[]{:S(2)}) async-start(s8[20971520]{0:T(1024)(128)(4,1)} %bitcast.354), calls=%async_computation.17 | async-start | bytes 8388608
  1492.7 12.3 slice-start.3
  1492.7 13.4 slice-start.4
Sparse Core Ops, SparseCore 0:
  376.0 129.7 reduce-scatter.28
  509.3 126.8 reduce-scatter.26
  640.3 126.8 reduce-scatter.24
  770.6 126.8 reduce-scatter.22
  901.5 126.8 reduce-scatter.18
  1032.4 126.8 reduce-scatter.20
  1161.1 101.8 all-gather.13
  1265.4 101.8 all-gather.11
  1369.7 101.8 all-gather.9
where the time goes:
time: 1530 us; the launch traced here: 1520 us
  waiting for transfers between devices  848 us (55%)
  matrix products  484 us (32%)
  other arithmetic  115 us (8%)
  local copies, waits for them, and re-layouts  59.2 us (4%)
    unnamed x15, waiting for transfers between devices  547 us
    reshape x3, waiting for transfers between devices, step(): t.reshape(-1, *t.shape[2:])  301 us
    dot_general x5, matrix products, layer(): up = jnp.dot(a, w['w_up'], preferred_element_type=jnp.float32)  165 us
    dot_general x5, matrix products, layer(): gate = jnp.dot(a, w['w_gate'], preferred_element_type=jnp.float32)  163 us
    dot_general x5, matrix products, matmul(): jnp.dot(a, w, preferred_element_type=jnp.float32).astype(jnp.bfloat16)  155 us
    unnamed x5, other arithmetic  72.9 us
    unnamed x37, local copies, waits for them, and re-layouts  59.2 us
  transfers between devices with their start and end apart: 9, of which 8 were waited for; matrix products, arithmetic and copies ran while one was open for 16% of the time, Pallas kernels for 0%

commit v1 on v0

v1 whole, which is shorter than its diff:
```python
import jax
import jax.numpy as jnp
from jax import lax
from jax.sharding import PartitionSpec as P

F32, BF16 = jnp.float32, jnp.bfloat16


def normed(h):
    wide = h.astype(F32)
    scale = lax.rsqrt(jnp.mean(wide**2, -1, keepdims=True) + 1e-6)
    return (wide * scale).astype(BF16)


def dot(a, b, dims):
    return lax.dot_general(a, b, (dims, ((), ())), preferred_element_type=F32)


NN, NT, TN = ((1,), (0,)), ((1,), (1,)), ((0,), (0,))


def up_part(a, wg, wu):
    gate = dot(a, wg, NN)
    up = dot(a, wu, NN)
    return gate, up, (jax.nn.silu(gate) * up).astype(BF16)


def through_product(gate, up, d):
    wide = d.astype(F32)
    s = jax.nn.sigmoid(gate)
    return (wide * up * (s * (1 + gate * (1 - s)))).astype(BF16), (wide * gate * s).astype(BF16)


def adamw(w, m, v, g):
    m = 0.9 * m + 0.1 * g
    v = 0.95 * v + 0.05 * g * g
    step = m * lax.rsqrt(v + 1e-8) + 0.1 * w
    return (w - 0.02 * step).astype(BF16), m, v


def solution(mesh):
    n = mesh.shape["dp"]

    def step(x, dy, w_gate, w_up, w_down, *moments):
        weights = (w_gate, w_up, w_down)
        x, dy = x[0], dy[0]
        me = lax.axis_index("dp")
        done = {}

        def scatter(term):
            return lax.psum_scatter(term.astype(BF16), "dp", scatter_dimension=0, tiled=True)

        def update(layer, which, g):
            w = weights[which][layer]
            rows = w.shape[0] // n
            own = lax.dynamic_slice_in_dim(w, me * rows, rows, 0).astype(F32)
            new, m, v = adamw(own, moments[which][layer], moments[3 + which][layer], g.astype(F32))
            done[layer, which] = lax.all_gather(new, "dp", axis=0, tiled=True), m, v

        a0 = normed(x)
        gate0, up0, act0 = up_part(a0, w_gate[0], w_up[0])
        h1 = x + dot(act0, w_down[0], NN).astype(BF16)
        a1, back1 = jax.vjp(normed, h1)
        gate1, up1, act1 = up_part(a1, w_gate[1], w_up[1])
        g_d1 = scatter(dot(act1, dy, TN))
        dact1 = dot(dy, w_down[1], NT).astype(BF16)
        dg1, du1 = through_product(gate1, up1, dact1)
        g_g1 = scatter(dot(a1, dg1, TN))
        g_u1 = scatter(dot(a1, du1, TN))
        da1 = dot(dg1, w_gate[1], NT).astype(BF16) + dot(du1, w_up[1], NT).astype(BF16)
        dh1 = dy + back1(da1)[0]
        g_d0 = scatter(dot(act0, dh1, TN))
        dact0 = dot(dh1, w_down[0], NT).astype(BF16)
        dg0, du0 = through_product(gate0, up0, dact0)
        g_g0 = scatter(dot(a0, dg0, TN))
        g_u0 = scatter(dot(a0, du0, TN))
        update(1, 2, g_d1)
        update(1, 0, g_g1)
        update(1, 1, g_u1)
        update(0, 2, g_d0)
        update(0, 0, g_g0)
        update(0, 1, g_u0)
        return tuple(jnp.stack([done[0, which][k], done[1, which][k]]) for k in range(3) for which in range(3))

    seq, whole, block, group = P(("rep", "dp"), None, None), P(None, None, None), P(None, "dp", None), P("rep", None, None)
    return jax.shard_map(
        step,
        mesh=mesh,
        in_specs=(seq, seq) + (whole,) * 3 + (block,) * 6,
        out_specs=(group,) * 3 + (P("rep", "dp", None),) * 6,
        check_vma=False,
    )
```

time: 1530 us -> 1140 us (0.75)
  waiting for transfers between devices: 848 us -> 444 us
    unnamed x15 -> x12, waiting for transfers between devices: 547 us -> 1.9 us
    reshape x3 -> x0, waiting for transfers between devices: 301 us -> none  [step(): t.reshape(-1, *t.shape[2:])]
    all_gather x0 -> x6, waiting for transfers between devices: none -> 288 us  [update(): done[layer, which] = (lax.all_gather(new, 'dp', axis=0, tiled=True), m, v)]
    reduce_scatter x0 -> x6, waiting for transfers between devices: none -> 154 us  [scatter(): lax.psum_scatter(term.astype(BF16), 'dp', scatter_dimension=0, tiled=True)]
    another operation x0 -> x6, other arithmetic: none -> 73.7 us  [step(): jnp.stack([done[0, which][k], done[1, which][k]])]
    unnamed x5 -> x0, other arithmetic: 72.9 us -> none
    slice x0 -> x3, local copies, waits for them, and re-layouts: none -> 48.5 us  [the longest x1 16.2 us: step(): gate0, up0, act0 = up_part(a0, w_gate[0], w_up[0])]
    unnamed x37 -> x28, local copies, waits for them, and re-layouts: 59.2 us -> 16.3 us
  transfers between devices with their start and end apart: 9 -> 12, of which waited for: 8 -> 9; matrix products, arithmetic and copies ran while one was open for 16% -> 35% of each run, Pallas kernels for 0% -> 0%
where the time goes in v1:
time: 1140 us; the launch traced here: 1130 us
  matrix products  488 us (43%)
  waiting for transfers between devices  444 us (39%)
  other arithmetic  120 us (11%)
  local copies, waits for them, and re-layouts  64.8 us (6%)
  between operations  14.8 us (1%)
    dot_general x15, matrix products, dot(): return lax.dot_general(a, b, (dims, ((), ())), preferred_element_type=F32)  488 us
    all_gather x6, waiting for transfers between devices, update(): done[layer, which] = (lax.all_gather(new, 'dp', axis=0, tiled=True), m, v)  288 us
    reduce_scatter x6, waiting for transfers between devices, scatter(): lax.psum_scatter(term.astype(BF16), 'dp', scatter_dimension=0, tiled=True)  154 us
    another operation x6, other arithmetic, step(): jnp.stack([done[0, which][k], done[1, which][k]])  73.7 us
    convert_element_type x3, other arithmetic, adamw(): return ((w - 0.02 * step).astype(BF16), m, v)  29.8 us
  transfers between devices with their start and end apart: 12, of which 9 were waited for; matrix products, arithmetic and copies ran while one was open for 35% of the time, Pallas kernels for 0%

profile of v1, /device:TPU:0, one launch (start us, length us, event | category | flops | bytes accessed | tf_op | source)
XLA Modules:
  0.0 1131.2 jit_solution(13698701435761948335)
XLA Ops:
  19.1 27.9 %fusion.40 = f32[2048,4096]{1,0:T(8,128)} fusion(bf16[1,2048,1280]{2,1,0:T(8,128)(2,1)S(1)} %copy-done.5, f32[2048]{0:T(1024)S(1)} %add_rsqrt_fusion, bf16[2,1280,4096]{2,1,0:T(8,128)(2,1)} %param.13), kind=kOutput, calls=%fused_computation.57 | convolution fusion | flops 21482700800 | bytes 49291264 | tf_op jit(solution)/shard_map/dot_general | solution.py:16
  47.0 41.5 %multiply_convert_fusion.1 = (bf16[2048,4096]{1,0:T(8,128)(2,1)}, f32[2048,4096]{1,0:T(8,128)}) fusion(f32[2048,4096]{1,0:T(8,128)} %fusion.40, bf16[2,1280,4096]{2,1,0:T(8,128)(2,1)} %param.14, bf16[1,2048,1280]{2,1,0:T(8,128)(2,1)} %param.11, f32[2048]{0:T(1024)S(1)} %add_rsqrt_fusion), kind=kOutput, calls=%fused_computation.14 | convolution fusion | flops 21533032448 | bytes 99622912 | tf_op jit(solution)/shard_map/dot_general | solution.py:16
  88.5 30.3 %fusion.24 = (f32[2048]{0:T(1024)S(1)}, bf16[2048,1280]{0,1:T(8,128)(2,1)}) fusion(bf16[2048,4096]{1,0:T(8,128)(2,1)} %get-tuple-element.35, bf16[2,4096,1280]{2,1,0:T(8,128)(2,1)} %param.15, bf16[1,2048,1280]{1,2,0:T(8,128)(2,1)} %copy.20), kind=kOutput, calls=%fused_computation.41 | convolution fusion | flops 21487941632 | bytes 37756928 | tf_op jit(solution)/shard_map/dot_general | solution.py:16
  118.8 28.9 %convolution_convert_fusion.4 = bf16[2048,4096]{1,0:T(8,128)(2,1)} fusion(bf16[1,2048,1280]{2,1,0:T(8,128)(2,1)} %param.12, bf16[2,4096,1280]{2,1,0:T(8,128)(2,1)} %param.15), kind=kOutput, calls=%fused_computation.33 | convolution fusion | flops 21483225088 | bytes 32505856 | tf_op jit(solution)/shard_map/dot_general | solution.py:16
  147.7 30.2 %fusion.33 = f32[2048,4096]{1,0:T(8,128)} fusion(bf16[2048,1280]{0,1:T(8,128)(2,1)} %get-tuple-element.38, f32[2048]{0:T(1024)S(1)} %fusion.112, bf16[2,1280,4096]{2,1,0:T(8,128)(2,1)} %param.14), kind=kOutput, calls=%fused_computation.50 | convolution fusion | flops 21482700800 | bytes 49291264 | tf_op jit(solution)/shard_map/dot_general | solution.py:16
  177.9 50.3 %fusion.3 = (bf16[2048,4096]{1,0:T(8,128)(2,1)}, bf16[2048,4096]{1,0:T(8,128)(2,1)}, f32[2048,4096]{1,0:T(8,128)}) fusion(bf16[2048,4096]{1,0:T(8,128)(2,1)} %convolution_convert_fusion.4, f32[2048,4096]{1,0:T(8,128)} %fusion.33, bf16[2,1280,4096]{2,1,0:T(8,128)(2,1)} %param.13, bf16[2048,1280]{0,1:T(8,128)(2,1)S(1)} %copy-done.6, f32[2048]{0:T(1024)S(1)} %fusion.112), kind=kOutput, calls=%fused_computation.7 | convolution fusion | flops 21600141312 | bytes 133177344 | tf_op jit(solution)/shard_map/dot_general | solution.py:16
  228.2 35.1 %fusion.16 = bf16[4096,1280]{1,0:T(8,128)(2,1)} fusion(f32[2048,4096]{1,0:T(8,128)} %fusion.33, f32[2048,4096]{1,0:T(8,128)} %get-tuple-element.39, bf16[1,2048,1280]{2,1,0:T(8,128)(2,1)} %param.12), kind=kOutput, calls=%fused_computation.27 | convolution fusion | flops 21530411008 | bytes 82837504 | tf_op jit(solution)/shard_map/dot_general | solution.py:16
  271.6 28.9 %fusion.46 = bf16[2048,1280]{0,1:T(8,128)(2,1)} fusion(bf16[2048,4096]{1,0:T(8,128)(2,1)} %get-tuple-element.9, bf16[2,1280,4096]{2,1,0:T(8,128)(2,1)} %param.14), kind=kOutput, calls=%fused_computation.62 | convolution fusion | flops 21477457920 | bytes 32505856 | tf_op jit(solution)/shard_map/dot_general | solution.py:16
  300.5 31.4 %fusion.26 = (f32[2048]{0:T(1024)S(1)}, bf16[2048,1280]{0,1:T(8,128)(2,1)}) fusion(bf16[2048,1280]{0,1:T(8,128)(2,1)} %get-tuple-element.38, bf16[2048,1280]{0,1:T(8,128)(2,1)} %fusion.46, bf16[2048,4096]{1,0:T(8,128)(2,1)} %get-tuple-element.10, bf16[2,1280,4096]{2,1,0:T(8,128)(2,1)} %param.13), kind=kOutput, calls=%fused_computation.43 | convolution fusion | flops 21490563072 | bytes 42999808 | tf_op jit(solution)/shard_map/dot_general | solution.py:16
  331.9 12.4 %fusion.59 = bf16[2048,1280]{0,1:T(8,128)(2,1)} fusion(bf16[2048,1280]{0,1:T(8,128)(2,1)} %get-tuple-element.38, bf16[2048,1280]{0,1:T(8,128)(2,1)} %get-tuple-element.41, bf16[1,2048,1280]{1,2,0:T(8,128)(2,1)} %copy.21, f32[2048]{0:T(1024)S(1)} %multiply_multiply_fusion.6, f32[2048]{0:T(1024)S(1)} %copy-done.8), kind=kLoop, calls=%fused_computation.67 | loop fusion | flops 18350080 | bytes 20987904 | tf_op jit(solution)/shard_map/add | solution.py:71
  344.3 28.1 %convolution_convert_fusion = bf16[4096,1280]{1,0:T(8,128)(2,1)} fusion(bf16[2048,4096]{1,0:T(8,128)(2,1)} %get-tuple-element.35, bf16[2048,1280]{0,1:T(8,128)(2,1)} %fusion.59), kind=kOutput, calls=%fused_computation.29 | convolution fusion | flops 21480079360 | bytes 32505856 | tf_op jit(solution)/shard_map/dot_general | solution.py:16
  372.5 27.7 %convolution_convert_fusion.1 = bf16[1280,4096]{1,0:T(8,128)(2,1)} fusion(bf16[2048,4096]{1,0:T(8,128)(2,1)} %get-tuple-element.9, bf16[2048,1280]{0,1:T(8,128)(2,1)} %get-tuple-element.38, f32[2048]{0:T(1024)S(1)} %copy-done.8), kind=kOutput, calls=%fused_computation.30 | convolution fusion | flops 21487943680 | bytes 32514048 | tf_op jit(solution)/shard_map/dot_general | solution.py:16
  400.3 29.3 %convolution_convert_fusion.3 = bf16[2048,4096]{1,0:T(8,128)(2,1)} fusion(bf16[2048,1280]{0,1:T(8,128)(2,1)} %fusion.59, bf16[2,4096,1280]{2,1,0:T(8,128)(2,1)} %param.15), kind=kOutput, calls=%fused_computation.32 | convolution fusion | flops 21483225088 | bytes 32505856 | tf_op jit(solution)/shard_map/dot_general | solution.py:16
  429.6 30.6 %fusion.17 = bf16[1280,4096]{1,0:T(8,128)(2,1)} fusion(f32[2048,4096]{1,0:T(8,128)} %fusion.40, bf16[2048,4096]{1,0:T(8,128)(2,1)} %convolution_convert_fusion.3, bf16[1,2048,1280]{1,2,0:T(8,128)(2,1)} %copy.20, f32[2048]{0:T(1024)S(1)} %copy-done.12), kind=kOutput, calls=%fused_computation.28 | convolution fusion | flops 21546663936 | bytes 66068480 | tf_op jit(solution)/shard_map/dot_general | solution.py:16
  460.2 28.0 %convolution_convert_fusion.2 = bf16[1280,4096]{1,0:T(8,128)(2,1)} fusion(bf16[2048,4096]{1,0:T(8,128)(2,1)} %get-tuple-element.10, bf16[2048,1280]{0,1:T(8,128)(2,1)} %get-tuple-element.38, f32[2048]{0:T(1024)S(1)} %copy-done.8), kind=kOutput, calls=%fused_computation.31 | convolution fusion | flops 21487943680 | bytes 32514048 | tf_op jit(solution)/shard_map/dot_general | solution.py:16
  488.3 39.9 %fusion.13 = bf16[1280,4096]{1,0:T(8,128)(2,1)} fusion(f32[2048,4096]{1,0:T(8,128)} %get-tuple-element.36, bf16[2048,4096]{1,0:T(8,128)(2,1)} %convolution_convert_fusion.3, f32[2048,4096]{1,0:T(8,128)} %fusion.40, bf16[1,2048,1280]{1,2,0:T(8,128)(2,1)} %copy.20, f32[2048]{0:T(1024)S(1)} %copy-done.12), kind=kOutput, calls=%fused_computation.26 | convolution fusion | flops 21580218368 | bytes 99622912 | tf_op jit(solution)/shard_map/dot_general | solution.py:16
  528.2 16.0 %fusion.125 = (bf16[1,4096,1280]{2,1,0:T(8,128)(2,1)}, bf16[1,4096,1280]{2,1,0:T(8,128)(2,1)}) fusion(bf16[2,4096,1280]{2,1,0:T(8,128)(2,1)} %param.15), kind=kLoop, calls=%fused_computation.158 | loop fusion | bytes 41943040 | tf_op jit(solution)/shard_map/slice | solution.py:62
  554.8 16.2 %fusion.126 = (bf16[1,1280,4096]{2,1,0:T(8,128)(2,1)}, bf16[1,1280,4096]{2,1,0:T(8,128)(2,1)}) fusion(bf16[2,1280,4096]{2,1,0:T(8,128)(2,1)} %param.14), kind=kLoop, calls=%fused_computation.159 | loop fusion | bytes 41943040 | tf_op jit(solution)/shard_map/slice | solution.py:61
  571.0 28.5 %reduce-scatter.11.cloned.1.call-done = bf16[160,4096]{1,0:T(8,128)(2,1)} async-done(((bf16[1280,4096]{1,0:T(8,128)(2,1)}), bf16[160,4096]{1,0:T(8,128)(2,1)}) %reduce-scatter.11.cloned.1.call-update) | async-done | bytes 1310736 | tf_op jit(solution)/shard_map/reduce_scatter | solution.py:51
  610.2 16.2 %fusion.127 = (bf16[1,1280,4096]{2,1,0:T(8,128)(2,1)}, bf16[1,1280,4096]{2,1,0:T(8,128)(2,1)}) fusion(bf16[2,1280,4096]{2,1,0:T(8,128)(2,1)} %param.13), kind=kLoop, calls=%fused_computation.160 | loop fusion | bytes 41943040 | tf_op jit(solution)/shard_map/slice | solution.py:54
  626.4 48.8 %reduce-scatter.9.cloned.1.call-done = bf16[160,4096]{1,0:T(8,128)(2,1)} async-done(((bf16[1280,4096]{1,0:T(8,128)(2,1)}), bf16[160,4096]{1,0:T(8,128)(2,1)}) %reduce-scatter.9.cloned.1.call-update) | async-done | bytes 1310736 | tf_op jit(solution)/shard_map/reduce_scatter | solution.py:51
  675.2 76.3 %reduce-scatter.7.cloned.1.call-done = bf16[160,4096]{1,0:T(8,128)(2,1)} async-done(((bf16[1280,4096]{1,0:T(8,128)(2,1)}), bf16[160,4096]{1,0:T(8,128)(2,1)}) %reduce-scatter.7.cloned.1.call-update) | async-done | bytes 1310736 | tf_op jit(solution)/shard_map/reduce_scatter | solution.py:51
  751.6 10.0 fusion.76
  784.4 26.4 %all-gather.15.cloned.1.call-done = bf16[4096,1280]{1,0:T(8,128)(2,1)} async-done(((bf16[512,1280]{1,0:T(8,128)(2,1)}), bf16[4096,1280]{1,0:T(8,128)(2,1)}) %all-gather.15.cloned.1.call-update) | async-done | bytes 10485776 | tf_op jit(solution)/shard_map/all_gather | solution.py:58
  810.8 59.2 %all-gather.17.cloned.1.call-done = bf16[4096,1280]{1,0:T(8,128)(2,1)} async-done(((bf16[512,1280]{1,0:T(8,128)(2,1)}), bf16[4096,1280]{1,0:T(8,128)(2,1)}) %all-gather.17.cloned.1.call-update) | async-done | bytes 10485776 | tf_op jit(solution)/shard_map/all_gather | solution.py:58
  870.1 17.3 %pad_maximum_fusion.2 = bf16[2,4096,1280]{2,1,0:T(8,128)(2,1)} fusion(bf16[1,4096,1280]{2,1,0:T(8,128)(2,1)} %bitcast.197, bf16[1,4096,1280]{2,1,0:T(8,128)(2,1)} %bitcast.196), kind=kLoop, calls=%fused_computation.18 | loop fusion | flops 10485760 | bytes 41943040 | tf_op jit(solution)/shard_map/stack | solution.py:83
  887.3 42.0 %all-gather.11.cloned.1.call-done = bf16[1280,4096]{1,0:T(8,128)(2,1)} async-done(((bf16[160,4096]{1,0:T(8,128)(2,1)}), bf16[1280,4096]{1,0:T(8,128)(2,1)}) %all-gather.11.cloned.1.call-update) | async-done | bytes 10485776 | tf_op jit(solution)/shard_map/all_gather | solution.py:58
  929.3 59.1 %all-gather.13.cloned.1.call-done = bf16[1280,4096]{1,0:T(8,128)(2,1)} async-done(((bf16[160,4096]{1,0:T(8,128)(2,1)}), bf16[1280,4096]{1,0:T(8,128)(2,1)}) %all-gather.13.cloned.1.call-update) | async-done | bytes 10485776 | tf_op jit(solution)/shard_map/all_gather | solution.py:58
  988.4 17.2 %pad_maximum_fusion.1 = bf16[2,1280,4096]{2,1,0:T(8,128)(2,1)} fusion(bf16[1,1280,4096]{2,1,0:T(8,128)(2,1)} %bitcast.199, bf16[1,1280,4096]{2,1,0:T(8,128)(2,1)} %bitcast.198), kind=kLoop, calls=%fused_computation.17 | loop fusion | flops 10485760 | bytes 41943040 | tf_op jit(solution)/shard_map/stack | solution.py:83
  1005.6 42.1 %all-gather.7.cloned.1.call-done = bf16[1280,4096]{1,0:T(8,128)(2,1)} async-done(((bf16[160,4096]{1,0:T(8,128)(2,1)}), bf16[1280,4096]{1,0:T(8,128)(2,1)}) %all-gather.7.cloned.1.call-update) | async-done | bytes 10485776 | tf_op jit(solution)/shard_map/all_gather | solution.py:58
  1047.7 59.1 %all-gather.9.cloned.1.call-done = bf16[1280,4096]{1,0:T(8,128)(2,1)} async-done(((bf16[160,4096]{1,0:T(8,128)(2,1)}), bf16[1280,4096]{1,0:T(8,128)(2,1)}) %all-gather.9.cloned.1.call-update) | async-done | bytes 10485776 | tf_op jit(solution)/shard_map/all_gather | solution.py:58
  1106.8 17.2 %pad_maximum_fusion = bf16[2,1280,4096]{2,1,0:T(8,128)(2,1)} fusion(bf16[1,1280,4096]{2,1,0:T(8,128)(2,1)} %bitcast.201, bf16[1,1280,4096]{2,1,0:T(8,128)(2,1)} %bitcast.200), kind=kLoop, calls=%fused_computation.16 | loop fusion | flops 10485760 | bytes 41943040 | tf_op jit(solution)/shard_map/stack | solution.py:83
  (64 shorter events, 64.3 us)
Async XLA Ops:
  7.2 537.1 %reduce-scatter.17.cloned.1.call-start = ((), (), s32[]{:S(2)}) async-start(), calls=%async_computation.16 | async-start | bytes 11796480 | tf_op jit(solution)/shard_map/reduce_scatter | solution.py:51
  15.1 4.0 copy-start.5
  19.1 27.9 %copy-start.11 = (f32[2048]{0:T(1024)}, f32[2048]{0:T(1024)S(1)}, u32[]{:S(2)}) copy-start(f32[2048]{0:T(1024)S(1)} %add_rsqrt_fusion) | copy-start | bytes 24580
  118.8 28.9 %copy-start.9 = (f32[2048]{0:T(1024)}, f32[2048]{0:T(1024)S(1)}, u32[]{:S(2)}) copy-start(f32[2048]{0:T(1024)S(1)} %get-tuple-element.37) | copy-start | bytes 24580
  118.8 59.1 %copy-start.7 = (f32[2048]{0:T(1024)}, f32[2048]{0:T(1024)S(1)}, u32[]{:S(2)}) copy-start(f32[2048]{0:T(1024)S(1)} %fusion.112) | copy-start | bytes 24580
  147.7 30.2 %copy-start.6 = (bf16[2048,1280]{0,1:T(8,128)(2,1)S(1)}, bf16[2048,1280]{0,1:T(8,128)(2,1)}, u32[]{:S(2)}) copy-start(bf16[2048,1280]{0,1:T(8,128)(2,1)} %get-tuple-element.38) | copy-start | bytes 15728644
  263.4 280.8 %reduce-scatter.15.cloned.1.call-start = ((), (), s32[]{:S(2)}) async-start(), calls=%async_computation.14 | async-start | bytes 11796480 | tf_op jit(solution)/shard_map/reduce_scatter | solution.py:51
  300.4 31.4 %copy-start.10 = (f32[2048]{0:T(1024)S(1)}, f32[2048]{0:T(1024)}, u32[]{:S(2)}) copy-start(f32[2048]{0:T(1024)} %copy-done.9) | copy-start | bytes 24580
  300.5 31.5 %copy-start.8 = (f32[2048]{0:T(1024)S(1)}, f32[2048]{0:T(1024)}, u32[]{:S(2)}) copy-start(f32[2048]{0:T(1024)} %copy-done.7) | copy-start | bytes 24580
  372.5 198.6 %reduce-scatter.13.cloned.1.call-start = ((), (), s32[]{:S(2)}) async-start(), calls=%async_computation.12 | async-start | bytes 11796480 | tf_op jit(solution)/shard_map/reduce_scatter | solution.py:51
  400.3 29.3 %copy-start.12 = (f32[2048]{0:T(1024)S(1)}, f32[2048]{0:T(1024)}, u32[]{:S(2)}) copy-start(f32[2048]{0:T(1024)} %copy-done.11) | copy-start | bytes 24580
  400.3 199.2 %reduce-scatter.11.cloned.1.call-start = ((), (), s32[]{:S(2)}) async-start(), calls=%async_computation.10 | async-start | bytes 11796480 | tf_op jit(solution)/shard_map/reduce_scatter | solution.py:51
  460.2 215.1 %reduce-scatter.9.cloned.1.call-start = ((), (), s32[]{:S(2)}) async-start(), calls=%async_computation.8 | async-start | bytes 11796480 | tf_op jit(solution)/shard_map/reduce_scatter | solution.py:51
  488.2 263.4 %reduce-scatter.7.cloned.1.call-start = ((), (), s32[]{:S(2)}) async-start(), calls=%async_computation.6 | async-start | bytes 11796480 | tf_op jit(solution)/shard_map/reduce_scatter | solution.py:51
  528.2 282.7 %all-gather.15.cloned.1.call-start = ((), (), s32[]{:S(2)}) async-start(), calls=%async_computation.15 | async-start | bytes 11796480 | tf_op jit(solution)/shard_map/all_gather | solution.py:58
  554.0 316.1 %all-gather.17.cloned.1.call-start = ((), (), s32[]{:S(2)}) async-start(), calls=%async_computation.17 | async-start | bytes 11796480 | tf_op jit(solution)/shard_map/all_gather | solution.py:58
  554.8 374.6 %all-gather.11.cloned.1.call-start = ((), (), s32[]{:S(2)}) async-start(), calls=%async_computation.11 | async-start | bytes 11796480 | tf_op jit(solution)/shard_map/all_gather | solution.py:58
  609.6 378.9 %all-gather.13.cloned.1.call-start = ((), (), s32[]{:S(2)}) async-start(), calls=%async_computation.13 | async-start | bytes 11796480 | tf_op jit(solution)/shard_map/all_gather | solution.py:58
  610.1 437.5 %all-gather.7.cloned.1.call-start = ((), (), s32[]{:S(2)}) async-start(), calls=%async_computation.7 | async-start | bytes 11796480 | tf_op jit(solution)/shard_map/all_gather | solution.py:58
  761.6 345.1 %all-gather.9.cloned.1.call-start = ((), (), s32[]{:S(2)}) async-start(), calls=%async_computation.9 | async-start | bytes 11796480 | tf_op jit(solution)/shard_map/all_gather | solution.py:58
  762.2 8.9 copy-start
  762.2 8.8 copy-start.1
  762.2 8.8 copy-start.2
  762.2 8.8 copy-start.3
  771.1 4.8 copy-start.4
Sparse Core Ops, SparseCore 0:
  263.5 75.2 reduce-scatter.16
  372.6 75.2 reduce-scatter.14
  451.3 72.4 reduce-scatter.12
  527.0 72.4 reduce-scatter.10
  602.8 72.4 reduce-scatter.8
  679.1 72.4 reduce-scatter.6
  753.4 57.4 all-gather.14
  812.6 57.3 all-gather.16
  871.9 57.3 all-gather.10
  931.0 57.3 all-gather.12
  990.2 57.3 all-gather.6
  1049.3 57.3 all-gather.8
